TPU v7x, 32 devices: a whole 2x2x4 slice. The times are simulated.
32 devices in a mesh: row: 16 (over z, x, core), chan: 2 (over y).
Axes of the slice: x: 2, y: 2, z: 4, core: 2. Of those that a mesh axis runs over, the one named last changes fastest.
Arguments:
- pair_rep: float32 [256, 256, 128], P('row', 'chan'), may hold values from -630 to 630
- residue_mask: int32 [256], replicated, may hold values from 0 to 1, as said below
- norm_gain: float32 [128], replicated, may hold values from 0.5 to 1.5
- norm_shift: float32 [128], replicated, may hold values from -3 to 3
- proj_weight: float32 [128, 512], replicated, may hold values from -4 to 4
- gate_shift: float32 [128], replicated, may hold values from -4 to 4
- bias_weight: float32 [128, 4], replicated, may hold values from -0.5 to 0.5
- out_weight: float32 [128, 128], replicated, may hold values from -0.5 to 0.5
Outputs:
- update: float32 [256, 256, 128], P('row', 'chan')
Inputs may be any that keep to these rules, and one draw needn't show every extreme that they name: `residue_mask`: residue 0 is always valid.
All inputs are finite; a program needn't handle non-finite values.
Results may differ from a plain program's by a relative error of at most 0.012.
Values may be sent and summed in bfloat16 or wider, within the bound.
No kernel may reach another device: no remote copies, remote signals or barrier semaphores. Data moves between devices by JAX's collectives and lax.ppermute only.
A program may use at most 64 MiB of HBM per device.

v0:
```python
import math
import jax
import jax.numpy as jnp
from jax import lax
from jax.sharding import PartitionSpec as P

C = 128
HEADS = 4


def normalize(values, norm_gain, norm_shift):
    average = jnp.mean(values, axis=-1, keepdims=True)
    centered = values - average
    variance = jnp.mean(centered * centered, axis=-1, keepdims=True)
    return centered * lax.rsqrt(variance + 1e-05) * norm_gain + norm_shift


def body(
    pair_rep, residue_mask, norm_gain, norm_shift, proj_weight, gate_shift, bias_weight, out_weight
):
    highest = lax.Precision.HIGHEST
    head_dim = C // HEADS
    scaling = 1.0 / math.sqrt(head_dim)
    pair_rows, span, width = pair_rep.shape
    normed = normalize(pair_rep, norm_gain, norm_shift)
    projected = jnp.einsum("rjc,ce->rje", normed, proj_weight, precision=highest)
    query_half = (
        (projected[:, :, :width] * scaling)
        .astype(jnp.bfloat16)
        .reshape(pair_rows, span, HEADS, head_dim)
    )
    key_half = projected[:, :, width : 2 * width].astype(jnp.bfloat16)
    value_half = projected[:, :, 2 * width : 3 * width].astype(jnp.bfloat16)
    gates = projected[:, :, 3 * width :]
    bias_local = jnp.einsum("rjc,ch->hrj", normed, bias_weight, precision=highest)
    bias_cols = lax.all_gather(bias_local, "row", axis=1, tiled=True)
    own_bias = lax.all_to_all(bias_cols, "chan", split_axis=1, concat_axis=2, tiled=True)
    valid_keys = residue_mask > 0
    key_all, value_all = (
        lax.all_gather(key_half, "chan", axis=1, tiled=True),
        lax.all_gather(value_half, "chan", axis=1, tiled=True),
    )

    def one_row(operands):
        queries, key_row, value_row = operands
        key_heads = key_row.reshape(-1, HEADS, head_dim)
        scores = (
            jnp.einsum("jhd,khd->hjk", queries, key_heads, preferred_element_type=jnp.float32)
            + own_bias
        )
        weights = jax.nn.softmax(
            jnp.where(valid_keys[None, None, :], scores, -1000000000.0), axis=-1
        )
        values = value_row.astype(jnp.float32).reshape(-1, HEADS, head_dim)
        return jnp.einsum("hjk,khd->jhd", weights, values, precision=highest)

    attended = lax.map(one_row, (query_half, key_all, value_all)).reshape(pair_rows, span, width)
    gated_rows = jax.nn.sigmoid(gates + gate_shift) * attended
    return jnp.einsum("rjd,dc->rjc", gated_rows, out_weight, precision=highest)


def solution(mesh):
    return jax.shard_map(
        body,
        mesh=mesh,
        in_specs=(P("row", "chan", None), P(), P(), P(), P(), P(), P(), P()),
        out_specs=P("row", "chan", None),
        check_vma=False,
    )
```

profile of v0, /device:TPU:0, one launch (start us, length us, event | category | flops | bytes accessed | tf_op | source)
XLA Modules:
  0.0 117.3 jit_solution(9026340137136260485)
XLA Ops:
  6.5 1.6 %reduce_sum.27 = f32[16,128]{1,0:T(8,128)S(1)} reduce(f32[16,128,128]{2,1,0:T(8,128)} %param.10, f32[]{:T(128)} %constant.8.clone.1), dimensions={2}, to_apply=%region_0.0 | reduce | flops 260096 | bytes 1056772 | tf_op jit(solution)/shard_map/reduce_sum | solution.py:12
  8.2 1.9 %multiply_reduce_fusion = f32[16,128]{1,0:T(8,128)S(1)} fusion(f32[16,128,128]{2,1,0:T(8,128)} %param.10, f32[16,128]{1,0:T(8,128)S(1)} %broadcast_multiply_fusion), kind=kLoop, calls=%fused_computation.24 | loop fusion | flops 784384 | bytes 1064960 | tf_op jit(solution)/shard_map/reduce_sum | solution.py:14
  10.1 6.7 %fusion.34 = (bf16[16,128,512]{2,1,0:T(8,128)(2,1)S(1)}, f32[16,128,512]{2,1,0:T(8,128)}) fusion(f32[128,512]{1,0:T(8,128)S(1)} %copy-done, f32[16,128,128]{2,1,0:T(8,128)} %param.10, f32[128]{0:T(128)} %param.13, f32[128]{0:T(128)} %param.12, f32[16,128]{1,0:T(8,128)S(1)} %add_rsqrt_fusion, f32[16,128]{1,0:T(8,128)S(1)} %broadcast_multiply_fusion), kind=kOutput, calls=%fused_computation.46 | convolution fusion | flops 1612709888 | bytes 7619584 | tf_op jit(solution)/shard_map/rjc,ce->rje/dot_general | solution.py:26
  16.9 1.3 %fusion.33 = (bf16[16,128,128]{2,1,0:T(8,128)(2,1)}, bf16[16,128,128]{2,1,0:T(8,128)(2,1)}) fusion(bf16[16,128,512]{2,1,0:T(8,128)(2,1)S(1)} %get-tuple-element.84), kind=kLoop, calls=%fused_computation.45 | loop fusion | bytes 2097152 | tf_op jit(solution)/shard_map/slice | solution.py:32
  19.0 1.6 %convolution_bitcast_fusion.1 = f32[4,16,128]{2,0,1:T(4,128)S(1)} fusion(f32[16,128,128]{2,1,0:T(8,128)S(1)} %copy-done.1, f32[128]{0:T(128)S(1)} %copy-done.2, f32[128]{0:T(128)S(1)} %copy-done.3, f32[16,128]{1,0:T(8,128)S(1)} %add_rsqrt_fusion, f32[16,128]{1,0:T(8,128)S(1)} %broadcast_multiply_fusion, f32[128,4]{0,1:T(4,128)S(1)} %copy-done.4), kind=kOutput, calls=%fused_computation.14 | convolution fusion | flops 13631488 | bytes 1100800 | tf_op jit(solution)/shard_map/rjc,ch->hrj/dot_general | solution.py:35
  20.6 26.0 %all_gather.11 = f32[4,256,128]{2,0,1:T(4,128)} all-gather(f32[4,16,128]{2,0,1:T(4,128)S(1)} %convolution_bitcast_fusion.1), channel_id=1, replica_groups=mesh['row'=16,'chan'=2] {'row'}, dimensions={1}, use_global_device_ids=true | all-gather | bytes 557056 | tf_op jit(solution)/shard_map/all_gather | solution.py:36
  46.5 3.5 %all-to-all-start = ((f32[4,256,128]{2,0,1:T(4,128)}), f32[4,256,128]{2,0,1:T(4,128)S(1)}, u32[]{:S(2)}, u32[]{:S(2)}) async-start(f32[4,256,128]{2,0,1:T(4,128)} %all_gather.11), calls=%async_computation | async-start | bytes 1048576 | tf_op jit(solution)/shard_map/all_to_all | solution.py:37
  50.0 1.4 %fusion.9 = bf16[16,128,128]{2,1,0:T(8,128)(2,1)S(1)} fusion(f32[16,128,512]{2,1,0:T(8,128)} %get-tuple-element.85), kind=kLoop, calls=%fused_computation.16 | loop fusion | flops 524288 | bytes 1572864 | tf_op jit(solution)/shard_map/convert_element_type | solution.py:29
  51.8 12.5 %all-to-all-done = f32[4,256,128]{2,0,1:T(4,128)S(1)} async-done(((f32[4,256,128]{2,0,1:T(4,128)}), f32[4,256,128]{2,0,1:T(4,128)S(1)}, u32[]{:S(2)}, u32[]{:S(2)}) %all-to-all-start) | async-done | bytes 524320 | tf_op jit(solution)/shard_map/all_to_all | solution.py:37
  65.2 5.1 %all-gather.5.cloned.1.call-done = bf16[16,256,128]{2,1,0:T(8,128)(2,1)} async-done(((bf16[16,128,128]{2,1,0:T(8,128)(2,1)}), bf16[16,256,128]{2,1,0:T(8,128)(2,1)}) %all-gather.5.cloned.1.call-update) | async-done | bytes 1048592 | tf_op jit(solution)/shard_map/all_gather | solution.py:40
  70.3 36.5 %while.10 = (s32[]{:T(128)}, f32[16,128,4,32]{1,3,2,0:T(8,128)S(1)}, bf16[16,256,128]{2,1,0:T(8,128)(2,1)}, pred[256]{0:T(512)(128)(4,1)S(1)}, bf16[16,128,4,32]...) while((s32[]{:T(128)}, ...), condition=%wide.region_5.6_spmd, body=%wide.region_2.5_spmd.sunk | while | flops 59636736 | bytes 2861665 | solution.py:57
  70.3 0.9 constant_dynamic-slice_fusion.3
  72.6 0.9 constant_dynamic-slice_fusion.3
  74.9 0.9 constant_dynamic-slice_fusion.3
  77.1 0.9 constant_dynamic-slice_fusion.3
  79.4 0.9 constant_dynamic-slice_fusion.3
  81.7 0.9 constant_dynamic-slice_fusion.3
  84.0 0.9 constant_dynamic-slice_fusion.3
  86.2 0.9 constant_dynamic-slice_fusion.3
  88.5 0.9 constant_dynamic-slice_fusion.3
  93.1 0.9 constant_dynamic-slice_fusion.3
  97.6 0.9 constant_dynamic-slice_fusion.3
  102.2 0.9 constant_dynamic-slice_fusion.3
  107.1 3.3 %fusion.15 = f32[16,128,128]{2,1,0:T(8,128)} fusion(f32[16,128,128]{2,1,0:T(8,128)S(1)} %copy.23, f32[16,128,512]{2,1,0:T(8,128)} %get-tuple-element.85, f32[128]{0:T(128)S(1)} %copy-done.7, f32[128,128]{1,0:T(8,128)S(1)} %copy-done.5), kind=kOutput, calls=%fused_computation.25 | convolution fusion | flops 403963904 | bytes 3211776 | tf_op jit(solution)/shard_map/rjd,dc->rjc/dot_general | solution.py:59
  (113 shorter events, 27.7 us)
Async XLA Ops:
  6.5 3.5 %copy-start = (f32[128,512]{1,0:T(8,128)S(1)}, f32[128,512]{1,0:T(8,128)}, u32[]{:S(2)}) copy-start(f32[128,512]{1,0:T(8,128)} %param.14) | copy-start | bytes 786436
  6.5 58.7 %all-gather.3.cloned.1.call-start = ((), (), s32[]{:S(2)}) async-start(), calls=%async_computation.1 | async-start | bytes 1572864 | tf_op jit(solution)/shard_map/all_gather | solution.py:41
  10.1 8.9 %copy-start.1 = (f32[16,128,128]{2,1,0:T(8,128)S(1)}, f32[16,128,128]{2,1,0:T(8,128)}, u32[]{:S(2)}) copy-start(f32[16,128,128]{2,1,0:T(8,128)} %param.10) | copy-start | bytes 3145732
  10.1 8.9 %copy-start.2 = (f32[128]{0:T(128)S(1)}, f32[128]{0:T(128)}, u32[]{:S(2)}) copy-start(f32[128]{0:T(128)} %param.13) | copy-start | bytes 1540
  10.1 8.9 %copy-start.3 = (f32[128]{0:T(128)S(1)}, f32[128]{0:T(128)}, u32[]{:S(2)}) copy-start(f32[128]{0:T(128)} %param.12) | copy-start | bytes 1540
  10.1 8.9 %copy-start.4 = (f32[128,4]{0,1:T(4,128)S(1)}, f32[128,4]{0,1:T(4,128)}, u32[]{:S(2)}) copy-start(f32[128,4]{0,1:T(4,128)} %param.16) | copy-start | bytes 6148
  16.9 34.9 %copy-start.6 = (s32[256]{0:T(256)S(1)}, s32[256]{0:T(256)}, u32[]{:S(2)}) copy-start(s32[256]{0:T(256)} %param.11) | copy-start | bytes 3076
  18.2 52.1 %all-gather.5.cloned.1.call-start = ((), (), s32[]{:S(2)}) async-start(), calls=%async_computation.2 | async-start | bytes 1572864 | tf_op jit(solution)/shard_map/all_gather | solution.py:40
  46.5 17.8 %all-to-all-start = ((f32[4,256,128]{2,0,1:T(4,128)}), f32[4,256,128]{2,0,1:T(4,128)S(1)}, u32[]{:S(2)}, u32[]{:S(2)}) async-start(f32[4,256,128]{2,0,1:T(4,128)} %all_gather.11), calls=%async_computation | async-start | bytes 1048576 | tf_op jit(solution)/shard_map/all_to_all | solution.py:37
  70.3 36.8 %copy-start.5 = (f32[128,128]{1,0:T(8,128)S(1)}, f32[128,128]{1,0:T(8,128)}, u32[]{:S(2)}) copy-start(f32[128,128]{1,0:T(8,128)} %param.17) | copy-start | bytes 196612
  70.3 36.8 %copy-start.7 = (f32[128]{0:T(128)S(1)}, f32[128]{0:T(128)}, u32[]{:S(2)}) copy-start(f32[128]{0:T(128)} %param.15) | copy-start | bytes 1540
Sparse Core Ops, SparseCore 0:
  18.3 23.9 all-gather.2
  43.9 26.3 all-gather.4
where the time goes:
time: 118 us; the launch traced here: 117 us
  blocking collectives  26 us (22%)
  matrix products  25.9 us (22%)
  local copies, waits for them, and re-layouts  20.5 us (17%)
  waiting for transfers between devices  18.3 us (16%)
  between operations  13.6 us (12%)
  other arithmetic  9.11 us (8%)
  starting transfers between devices  3.53 us (3%)
    all_gather x1, blocking collectives, body(): bias_cols = lax.all_gather(bias_local, 'row', axis=1, tiled=True)  26 us
    dynamic_slice x48, local copies, waits for them, and re-layouts, body(): lax.map(one_row, (query_half, key_all, value_all))  17.7 us
    all_to_all x1, waiting for transfers between devices, body(): lax.all_to_all(bias_cols, 'chan', split_axis=1, concat_axis=2, tiled=True)  12.5 us
    dot_general x16, matrix products, one_row(): return jnp.einsum('hjk,khd->jhd', weights, values, precision=highest)  8.53 us
    dot_general x1, matrix products, body(): jnp.einsum('rjc,ce->rje', normed, proj_weight, precision=highest)  6.75 us
    dot_general x16, matrix products, one_row(): jnp.einsum('jhd,khd->hjk', queries, key_heads, preferred_element_type=jnp...  5.72 us
    all_gather x1, waiting for transfers between devices, body(): lax.all_gather(key_half, 'chan', axis=1, tiled=True)  5.06 us
    reduce_sum x16, other arithmetic, one_row(): jax.nn.softmax(jnp.where(valid_keys[None, None, :], scores, -1000000000.0...  4.19 us
  transfers between devices with their start and end apart: 3, of which 2 were waited for; matrix products, arithmetic and copies ran while one was open for 3% of the time, Pallas kernels for 0%

commit v1 on v0

--- a/solution.py
+++ b/solution.py
@@ -6,6 +6,17 @@
 
 C = 128
 HEADS = 4
+
+
+def turned_line(x, name, d):
+    count = lax.axis_size(name)
+    right = [(i, (i + 1) % count) for i in range(count)]
+    parts = [x]
+    for hop in range(1, count):
+        parts = [lax.ppermute(parts[0], name, right), *parts]
+    full = jnp.concatenate(parts, axis=d)
+    turn = (lax.axis_index(name) + 1) * parts[-1].shape[d]
+    return jnp.roll(full, turn, axis=d)
 
 
 def normalize(values, norm_gain, norm_shift):
@@ -33,7 +44,7 @@
     value_half = projected[:, :, 2 * width : 3 * width].astype(jnp.bfloat16)
     gates = projected[:, :, 3 * width :]
     bias_local = jnp.einsum("rjc,ch->hrj", normed, bias_weight, precision=highest)
-    bias_cols = lax.all_gather(bias_local, "row", axis=1, tiled=True)
+    bias_cols = turned_line(bias_local, "row", 1)
     own_bias = lax.all_to_all(bias_cols, "chan", split_axis=1, concat_axis=2, tiled=True)
     valid_keys = residue_mask > 0
     key_all, value_all = (

time: 118 us -> 180 us (1.53)
  waiting for transfers between devices: 18.3 us -> 104 us
  blocking collectives: 26 us -> 0 us
    ppermute x0 -> x15, waiting for transfers between devices: none -> 91 us  [turned_line(): parts = [lax.ppermute(parts[0], name, right), *parts]]
    all_gather x1 -> x0, blocking collectives: 26 us -> none  [body(): bias_cols = lax.all_gather(bias_local, 'row', axis=1, tiled=True)]
    all_gather x1, waiting for transfers between devices: 5.06 us -> 2.11 us  [body(): lax.all_gather(key_half, 'chan', axis=1, tiled=True)]
    all_to_all x1, waiting for transfers between devices: 12.5 us -> 10.6 us  [body(): lax.all_to_all(bias_cols, 'chan', split_axis=1, concat_axis=2, tiled=True)]
  transfers between devices with their start and end apart: 3 -> 18, of which waited for: 2 -> 17; matrix products, arithmetic and copies ran while one was open for 3% -> 3% of each run, Pallas kernels for 0% -> 0%
where the time goes in v1:
time: 180 us; the launch traced here: 179 us
  waiting for transfers between devices  104 us (58%)
  matrix products  25.9 us (14%)
  local copies, waits for them, and re-layouts  21.6 us (12%)
  between operations  13.8 us (8%)
  other arithmetic  9.03 us (5%)
  starting transfers between devices  4.13 us (2%)
    ppermute x15, waiting for transfers between devices, turned_line(): parts = [lax.ppermute(parts[0], name, right), *parts]  91 us
    dynamic_slice x48, local copies, waits for them, and re-layouts, body(): lax.map(one_row, (query_half, key_all, value_all))  17.7 us
    all_to_all x1, waiting for transfers between devices, body(): lax.all_to_all(bias_cols, 'chan', split_axis=1, concat_axis=2, tiled=True)  10.6 us
    dot_general x16, matrix products, one_row(): return jnp.einsum('hjk,khd->jhd', weights, values, precision=highest)  8.53 us
    dot_general x1, matrix products, body(): jnp.einsum('rjc,ce->rje', normed, proj_weight, precision=highest)  6.75 us
    dot_general x16, matrix products, one_row(): jnp.einsum('jhd,khd->hjk', queries, key_heads, preferred_element_type=jnp...  5.72 us
    reduce_sum x16, other arithmetic, one_row(): jax.nn.softmax(jnp.where(valid_keys[None, None, :], scores, -1000000000.0...  4.19 us
  transfers between devices with their start and end apart: 18, of which 17 were waited for; matrix products, arithmetic and copies ran while one was open for 3% of the time, Pallas kernels for 0%

profile of v1, /device:TPU:0, one launch (start us, length us, event | category | flops | bytes accessed | tf_op | source)
XLA Modules:
  0.0 178.6 jit_solution(12776692112356560990)
XLA Ops:
  6.5 1.6 reduce_sum.27
  8.2 1.9 %multiply_reduce_fusion = f32[16,128]{1,0:T(8,128)S(1)} fusion(f32[16,128,128]{2,1,0:T(8,128)} %param.10, f32[16,128]{1,0:T(8,128)S(1)} %broadcast_multiply_fusion), kind=kLoop, calls=%fused_computation.24 | loop fusion | flops 784384 | bytes 1064960 | tf_op jit(solution)/shard_map/reduce_sum | solution.py:25
  10.1 6.7 %fusion.34 = (bf16[16,128,512]{2,1,0:T(8,128)(2,1)S(1)}, f32[16,128,512]{2,1,0:T(8,128)}) fusion(f32[128,512]{1,0:T(8,128)S(1)} %copy-done, f32[16,128,128]{2,1,0:T(8,128)} %param.10, f32[128]{0:T(128)} %param.13, f32[128]{0:T(128)} %param.12, f32[16,128]{1,0:T(8,128)S(1)} %add_rsqrt_fusion, f32[16,128]{1,0:T(8,128)S(1)} %broadcast_multiply_fusion), kind=kOutput, calls=%fused_computation.79 | convolution fusion | flops 1612709888 | bytes 7619584 | tf_op jit(solution)/shard_map/rjc,ce->rje/dot_general | solution.py:37
  18.2 1.6 convolution_bitcast_fusion.1
  20.4 6.6 %collective-permute-done = f32[4,16,128]{2,0,1:T(4,128)S(1)} collective-permute-done((f32[4,16,128]{2,0,1:T(4,128)S(1)}, f32[4,16,128]{2,0,1:T(4,128)S(1)}, u32[]{:S(2)}, u32[]{:S(2)}) %collective-permute-start) | collective-permute-done | bytes 32800 | tf_op jit(solution)/shard_map/ppermute | solution.py:16
  26.9 6.0 %collective-permute-done.1 = f32[4,16,128]{2,0,1:T(4,128)S(1)} collective-permute-done((f32[4,16,128]{2,0,1:T(4,128)S(1)}, f32[4,16,128]{2,0,1:T(4,128)S(1)}, u32[]{:S(2)}, u32[]{:S(2)}) %collective-permute-start.1) | collective-permute-done | bytes 32800 | tf_op jit(solution)/shard_map/ppermute | solution.py:16
  33.0 6.0 %collective-permute-done.2 = f32[4,16,128]{2,0,1:T(4,128)S(1)} collective-permute-done((f32[4,16,128]{2,0,1:T(4,128)S(1)}, f32[4,16,128]{2,0,1:T(4,128)S(1)}, u32[]{:S(2)}, u32[]{:S(2)}) %collective-permute-start.2) | collective-permute-done | bytes 32800 | tf_op jit(solution)/shard_map/ppermute | solution.py:16
  39.0 6.0 %collective-permute-done.3 = f32[4,16,128]{2,0,1:T(4,128)S(1)} collective-permute-done((f32[4,16,128]{2,0,1:T(4,128)S(1)}, f32[4,16,128]{2,0,1:T(4,128)S(1)}, u32[]{:S(2)}, u32[]{:S(2)}) %collective-permute-start.3) | collective-permute-done | bytes 32800 | tf_op jit(solution)/shard_map/ppermute | solution.py:16
  45.1 6.0 %collective-permute-done.4 = f32[4,16,128]{2,0,1:T(4,128)S(1)} collective-permute-done((f32[4,16,128]{2,0,1:T(4,128)S(1)}, f32[4,16,128]{2,0,1:T(4,128)S(1)}, u32[]{:S(2)}, u32[]{:S(2)}) %collective-permute-start.4) | collective-permute-done | bytes 32800 | tf_op jit(solution)/shard_map/ppermute | solution.py:16
  51.1 6.0 %collective-permute-done.5 = f32[4,16,128]{2,0,1:T(4,128)S(1)} collective-permute-done((f32[4,16,128]{2,0,1:T(4,128)S(1)}, f32[4,16,128]{2,0,1:T(4,128)S(1)}, u32[]{:S(2)}, u32[]{:S(2)}) %collective-permute-start.5) | collective-permute-done | bytes 32800 | tf_op jit(solution)/shard_map/ppermute | solution.py:16
  57.1 6.0 %collective-permute-done.6 = f32[4,16,128]{2,0,1:T(4,128)S(1)} collective-permute-done((f32[4,16,128]{2,0,1:T(4,128)S(1)}, f32[4,16,128]{2,0,1:T(4,128)S(1)}, u32[]{:S(2)}, u32[]{:S(2)}) %collective-permute-start.6) | collective-permute-done | bytes 32800 | tf_op jit(solution)/shard_map/ppermute | solution.py:16
  63.2 6.0 %collective-permute-done.7 = f32[4,16,128]{2,0,1:T(4,128)S(1)} collective-permute-done((f32[4,16,128]{2,0,1:T(4,128)S(1)}, f32[4,16,128]{2,0,1:T(4,128)S(1)}, u32[]{:S(2)}, u32[]{:S(2)}) %collective-permute-start.7) | collective-permute-done | bytes 32800 | tf_op jit(solution)/shard_map/ppermute | solution.py:16
  69.2 6.0 %collective-permute-done.8 = f32[4,16,128]{2,0,1:T(4,128)S(1)} collective-permute-done((f32[4,16,128]{2,0,1:T(4,128)S(1)}, f32[4,16,128]{2,0,1:T(4,128)S(1)}, u32[]{:S(2)}, u32[]{:S(2)}) %collective-permute-start.8) | collective-permute-done | bytes 32800 | tf_op jit(solution)/shard_map/ppermute | solution.py:16
  75.2 6.0 %collective-permute-done.9 = f32[4,16,128]{2,0,1:T(4,128)S(1)} collective-permute-done((f32[4,16,128]{2,0,1:T(4,128)S(1)}, f32[4,16,128]{2,0,1:T(4,128)S(1)}, u32[]{:S(2)}, u32[]{:S(2)}) %collective-permute-start.9) | collective-permute-done | bytes 32800 | tf_op jit(solution)/shard_map/ppermute | solution.py:16
  81.3 6.0 %collective-permute-done.10 = f32[4,16,128]{2,0,1:T(4,128)S(1)} collective-permute-done((f32[4,16,128]{2,0,1:T(4,128)S(1)}, f32[4,16,128]{2,0,1:T(4,128)S(1)}, u32[]{:S(2)}, u32[]{:S(2)}) %collective-permute-start.10) | collective-permute-done | bytes 32800 | tf_op jit(solution)/shard_map/ppermute | solution.py:16
  87.3 6.0 %collective-permute-done.11 = f32[4,16,128]{2,0,1:T(4,128)S(1)} collective-permute-done((f32[4,16,128]{2,0,1:T(4,128)S(1)}, f32[4,16,128]{2,0,1:T(4,128)S(1)}, u32[]{:S(2)}, u32[]{:S(2)}) %collective-permute-start.11) | collective-permute-done | bytes 32800 | tf_op jit(solution)/shard_map/ppermute | solution.py:16
  93.4 6.0 %collective-permute-done.12 = f32[4,16,128]{2,0,1:T(4,128)S(1)} collective-permute-done((f32[4,16,128]{2,0,1:T(4,128)S(1)}, f32[4,16,128]{2,0,1:T(4,128)S(1)}, u32[]{:S(2)}, u32[]{:S(2)}) %collective-permute-start.12) | collective-permute-done | bytes 32800 | tf_op jit(solution)/shard_map/ppermute | solution.py:16
  99.4 6.0 %collective-permute-done.13 = f32[4,16,128]{2,0,1:T(4,128)S(1)} collective-permute-done((f32[4,16,128]{2,0,1:T(4,128)S(1)}, f32[4,16,128]{2,0,1:T(4,128)S(1)}, u32[]{:S(2)}, u32[]{:S(2)}) %collective-permute-start.13) | collective-permute-done | bytes 32800 | tf_op jit(solution)/shard_map/ppermute | solution.py:16
  105.5 6.0 %collective-permute-done.14 = f32[4,16,128]{2,0,1:T(4,128)S(1)} collective-permute-done((f32[4,16,128]{2,0,1:T(4,128)S(1)}, f32[4,16,128]{2,0,1:T(4,128)S(1)}, u32[]{:S(2)}, u32[]{:S(2)}) %collective-permute-start.14) | collective-permute-done | bytes 32800 | tf_op jit(solution)/shard_map/ppermute | solution.py:16
  112.8 3.5 %all-to-all-start = ((f32[4,256,128]{2,0,1:T(4,128)}), f32[4,256,128]{2,0,1:T(4,128)S(1)}, u32[]{:S(2)}, u32[]{:S(2)}) async-start(f32[4,256,128]{2,0,1:T(4,128)} %constant_dynamic-slice_fusion.2), calls=%async_computation | async-start | bytes 1048576 | tf_op jit(solution)/shard_map/all_to_all | solution.py:48
  118.0 10.6 %all-to-all-done = f32[4,256,128]{2,0,1:T(4,128)S(1)} async-done(((f32[4,256,128]{2,0,1:T(4,128)}), f32[4,256,128]{2,0,1:T(4,128)S(1)}, u32[]{:S(2)}, u32[]{:S(2)}) %all-to-all-start) | async-done | bytes 524320 | tf_op jit(solution)/shard_map/all_to_all | solution.py:48
  129.5 2.1 %all-gather.5.cloned.1.call-done = bf16[16,256,128]{2,1,0:T(8,128)(2,1)} async-done(((bf16[16,128,128]{2,1,0:T(8,128)(2,1)}), bf16[16,256,128]{2,1,0:T(8,128)(2,1)}) %all-gather.5.cloned.1.call-update) | async-done | bytes 1048592 | tf_op jit(solution)/shard_map/all_gather | solution.py:51
  131.6 36.5 %while.10 = (s32[]{:T(128)}, f32[16,128,4,32]{1,3,2,0:T(8,128)S(1)}, bf16[16,256,128]{2,1,0:T(8,128)(2,1)}, pred[256]{0:T(512)(128)(4,1)S(1)}, bf16[16,128,4,32]...) while((s32[]{:T(128)}, ...), condition=%wide.region_5.6_spmd, body=%wide.region_2.5_spmd.sunk | while | flops 59636736 | bytes 2861665 | solution.py:68
  168.4 3.3 %fusion.15 = f32[16,128,128]{2,1,0:T(8,128)} fusion(f32[16,128,128]{2,1,0:T(8,128)S(1)} %copy.18, f32[16,128,512]{2,1,0:T(8,128)} %get-tuple-element.78, f32[128]{0:T(128)S(1)} %copy-done.7, f32[128,128]{1,0:T(8,128)S(1)} %copy-done.5), kind=kOutput, calls=%fused_computation.25 | convolution fusion | flops 403963904 | bytes 3211776 | tf_op jit(solution)/shard_map/rjd,dc->rjc/dot_general | solution.py:70
  (175 shorter events, 42.1 us)
Async XLA Ops:
  6.5 122.9 %all-gather.3.cloned.1.call-start = ((), (), s32[]{:S(2)}) async-start(), calls=%async_computation.1 | async-start | bytes 1572864 | tf_op jit(solution)/shard_map/all_gather | solution.py:52
  10.1 8.2 %copy-start.1 = (f32[16,128,128]{2,1,0:T(8,128)S(1)}, f32[16,128,128]{2,1,0:T(8,128)}, u32[]{:S(2)}) copy-start(f32[16,128,128]{2,1,0:T(8,128)} %param.10) | copy-start | bytes 3145732
  10.1 8.2 %copy-start.2 = (f32[128]{0:T(128)S(1)}, f32[128]{0:T(128)}, u32[]{:S(2)}) copy-start(f32[128]{0:T(128)} %param.13) | copy-start | bytes 1540
  10.1 8.1 %copy-start.3 = (f32[128]{0:T(128)S(1)}, f32[128]{0:T(128)}, u32[]{:S(2)}) copy-start(f32[128]{0:T(128)} %param.12) | copy-start | bytes 1540
  18.1 99.8 %copy-start.6 = (s32[256]{0:T(256)S(1)}, s32[256]{0:T(256)}, u32[]{:S(2)}) copy-start(s32[256]{0:T(256)} %param.11) | copy-start | bytes 3076
  18.2 113.4 %all-gather.5.cloned.1.call-start = ((), (), s32[]{:S(2)}) async-start(), calls=%async_computation.2 | async-start | bytes 1572864 | tf_op jit(solution)/shard_map/all_gather | solution.py:51
  19.9 7.1 %collective-permute-start = (f32[4,16,128]{2,0,1:T(4,128)S(1)}, f32[4,16,128]{2,0,1:T(4,128)S(1)}, u32[]{:S(2)}, u32[]{:S(2)}) collective-permute-start(f32[4,16,128]{2,0,1:T(4,128)S(1)} %convolution_bitcast_fusion.1), channel_id=1, source_target_pairs={{0,2},{2,4},{4,6},{6,8},{8,10},{10,12},{12,14},{14,16},{16,18},{18... | collective-permute-start | bytes 98312 | tf_op jit(solution)/shard_map/ppermute | solution.py:16
  26.9 6.0 %collective-permute-start.1 = (f32[4,16,128]{2,0,1:T(4,128)S(1)}, f32[4,16,128]{2,0,1:T(4,128)S(1)}, u32[]{:S(2)}, u32[]{:S(2)}) collective-permute-start(f32[4,16,128]{2,0,1:T(4,128)S(1)} %collective-permute-done), channel_id=1, source_target_pairs={{0,2},{2,4},{4,6},{6,8},{8,10},{10,12},{12,14},{14,16},{16,18},{18... | collective-permute-start | bytes 98312 | tf_op jit(solution)/shard_map/ppermute | solution.py:16
  33.0 6.0 %collective-permute-start.2 = (f32[4,16,128]{2,0,1:T(4,128)S(1)}, f32[4,16,128]{2,0,1:T(4,128)S(1)}, u32[]{:S(2)}, u32[]{:S(2)}) collective-permute-start(f32[4,16,128]{2,0,1:T(4,128)S(1)} %collective-permute-done.1), channel_id=1, source_target_pairs={{0,2},{2,4},{4,6},{6,8},{8,10},{10,12},{12,14},{14,16},{16,18},{18... | collective-permute-start | bytes 98312 | tf_op jit(solution)/shard_map/ppermute | solution.py:16
  39.0 6.0 %collective-permute-start.3 = (f32[4,16,128]{2,0,1:T(4,128)S(1)}, f32[4,16,128]{2,0,1:T(4,128)S(1)}, u32[]{:S(2)}, u32[]{:S(2)}) collective-permute-start(f32[4,16,128]{2,0,1:T(4,128)S(1)} %collective-permute-done.2), channel_id=1, source_target_pairs={{0,2},{2,4},{4,6},{6,8},{8,10},{10,12},{12,14},{14,16},{16,18},{18... | collective-permute-start | bytes 98312 | tf_op jit(solution)/shard_map/ppermute | solution.py:16
  45.1 6.0 %collective-permute-start.4 = (f32[4,16,128]{2,0,1:T(4,128)S(1)}, f32[4,16,128]{2,0,1:T(4,128)S(1)}, u32[]{:S(2)}, u32[]{:S(2)}) collective-permute-start(f32[4,16,128]{2,0,1:T(4,128)S(1)} %collective-permute-done.3), channel_id=1, source_target_pairs={{0,2},{2,4},{4,6},{6,8},{8,10},{10,12},{12,14},{14,16},{16,18},{18... | collective-permute-start | bytes 98312 | tf_op jit(solution)/shard_map/ppermute | solution.py:16
  51.1 6.0 %collective-permute-start.5 = (f32[4,16,128]{2,0,1:T(4,128)S(1)}, f32[4,16,128]{2,0,1:T(4,128)S(1)}, u32[]{:S(2)}, u32[]{:S(2)}) collective-permute-start(f32[4,16,128]{2,0,1:T(4,128)S(1)} %collective-permute-done.4), channel_id=1, source_target_pairs={{0,2},{2,4},{4,6},{6,8},{8,10},{10,12},{12,14},{14,16},{16,18},{18... | collective-permute-start | bytes 98312 | tf_op jit(solution)/shard_map/ppermute | solution.py:16
  57.1 6.0 %collective-permute-start.6 = (f32[4,16,128]{2,0,1:T(4,128)S(1)}, f32[4,16,128]{2,0,1:T(4,128)S(1)}, u32[]{:S(2)}, u32[]{:S(2)}) collective-permute-start(f32[4,16,128]{2,0,1:T(4,128)S(1)} %collective-permute-done.5), channel_id=1, source_target_pairs={{0,2},{2,4},{4,6},{6,8},{8,10},{10,12},{12,14},{14,16},{16,18},{18... | collective-permute-start | bytes 98312 | tf_op jit(solution)/shard_map/ppermute | solution.py:16
  63.2 6.0 %collective-permute-start.7 = (f32[4,16,128]{2,0,1:T(4,128)S(1)}, f32[4,16,128]{2,0,1:T(4,128)S(1)}, u32[]{:S(2)}, u32[]{:S(2)}) collective-permute-start(f32[4,16,128]{2,0,1:T(4,128)S(1)} %collective-permute-done.6), channel_id=1, source_target_pairs={{0,2},{2,4},{4,6},{6,8},{8,10},{10,12},{12,14},{14,16},{16,18},{18... | collective-permute-start | bytes 98312 | tf_op jit(solution)/shard_map/ppermute | solution.py:16
  69.2 6.0 %collective-permute-start.8 = (f32[4,16,128]{2,0,1:T(4,128)S(1)}, f32[4,16,128]{2,0,1:T(4,128)S(1)}, u32[]{:S(2)}, u32[]{:S(2)}) collective-permute-start(f32[4,16,128]{2,0,1:T(4,128)S(1)} %collective-permute-done.7), channel_id=1, source_target_pairs={{0,2},{2,4},{4,6},{6,8},{8,10},{10,12},{12,14},{14,16},{16,18},{18... | collective-permute-start | bytes 98312 | tf_op jit(solution)/shard_map/ppermute | solution.py:16
  75.2 6.0 %collective-permute-start.9 = (f32[4,16,128]{2,0,1:T(4,128)S(1)}, f32[4,16,128]{2,0,1:T(4,128)S(1)}, u32[]{:S(2)}, u32[]{:S(2)}) collective-permute-start(f32[4,16,128]{2,0,1:T(4,128)S(1)} %collective-permute-done.8), channel_id=1, source_target_pairs={{0,2},{2,4},{4,6},{6,8},{8,10},{10,12},{12,14},{14,16},{16,18},{18... | collective-permute-start | bytes 98312 | tf_op jit(solution)/shard_map/ppermute | solution.py:16
  81.3 6.0 %collective-permute-start.10 = (f32[4,16,128]{2,0,1:T(4,128)S(1)}, f32[4,16,128]{2,0,1:T(4,128)S(1)}, u32[]{:S(2)}, u32[]{:S(2)}) collective-permute-start(f32[4,16,128]{2,0,1:T(4,128)S(1)} %collective-permute-done.9), channel_id=1, source_target_pairs={{0,2},{2,4},{4,6},{6,8},{8,10},{10,12},{12,14},{14,16},{16,18},{18... | collective-permute-start | bytes 98312 | tf_op jit(solution)/shard_map/ppermute | solution.py:16
  87.3 6.0 %collective-permute-start.11 = (f32[4,16,128]{2,0,1:T(4,128)S(1)}, f32[4,16,128]{2,0,1:T(4,128)S(1)}, u32[]{:S(2)}, u32[]{:S(2)}) collective-permute-start(f32[4,16,128]{2,0,1:T(4,128)S(1)} %collective-permute-done.10), channel_id=1, source_target_pairs={{0,2},{2,4},{4,6},{6,8},{8,10},{10,12},{12,14},{14,16},{16,18},{18... | collective-permute-start | bytes 98312 | tf_op jit(solution)/shard_map/ppermute | solution.py:16
  93.4 6.0 %collective-permute-start.12 = (f32[4,16,128]{2,0,1:T(4,128)S(1)}, f32[4,16,128]{2,0,1:T(4,128)S(1)}, u32[]{:S(2)}, u32[]{:S(2)}) collective-permute-start(f32[4,16,128]{2,0,1:T(4,128)S(1)} %collective-permute-done.11), channel_id=1, source_target_pairs={{0,2},{2,4},{4,6},{6,8},{8,10},{10,12},{12,14},{14,16},{16,18},{18... | collective-permute-start | bytes 98312 | tf_op jit(solution)/shard_map/ppermute | solution.py:16
  99.4 6.0 %collective-permute-start.13 = (f32[4,16,128]{2,0,1:T(4,128)S(1)}, f32[4,16,128]{2,0,1:T(4,128)S(1)}, u32[]{:S(2)}, u32[]{:S(2)}) collective-permute-start(f32[4,16,128]{2,0,1:T(4,128)S(1)} %collective-permute-done.12), channel_id=1, source_target_pairs={{0,2},{2,4},{4,6},{6,8},{8,10},{10,12},{12,14},{14,16},{16,18},{18... | collective-permute-start | bytes 98312 | tf_op jit(solution)/shard_map/ppermute | solution.py:16
  105.4 6.0 %collective-permute-start.14 = (f32[4,16,128]{2,0,1:T(4,128)S(1)}, f32[4,16,128]{2,0,1:T(4,128)S(1)}, u32[]{:S(2)}, u32[]{:S(2)}) collective-permute-start(f32[4,16,128]{2,0,1:T(4,128)S(1)} %collective-permute-done.13), channel_id=1, source_target_pairs={{0,2},{2,4},{4,6},{6,8},{8,10},{10,12},{12,14},{14,16},{16,18},{18... | collective-permute-start | bytes 98312 | tf_op jit(solution)/shard_map/ppermute | solution.py:16
  112.8 15.8 %all-to-all-start = ((f32[4,256,128]{2,0,1:T(4,128)}), f32[4,256,128]{2,0,1:T(4,128)S(1)}, u32[]{:S(2)}, u32[]{:S(2)}) async-start(f32[4,256,128]{2,0,1:T(4,128)} %constant_dynamic-slice_fusion.2), calls=%async_computation | async-start | bytes 1048576 | tf_op jit(solution)/shard_map/all_to_all | solution.py:48
  131.6 36.8 %copy-start.5 = (f32[128,128]{1,0:T(8,128)S(1)}, f32[128,128]{1,0:T(8,128)}, u32[]{:S(2)}) copy-start(f32[128,128]{1,0:T(8,128)} %param.17) | copy-start | bytes 196612
  131.6 36.8 %copy-start.7 = (f32[128]{0:T(128)S(1)}, f32[128]{0:T(128)}, u32[]{:S(2)}) copy-start(f32[128]{0:T(128)} %param.15) | copy-start | bytes 1540
  (2 other events, 11.7 us)
Sparse Core Ops, SparseCore 0:
  18.3 23.9 all-gather.2
  105.6 25.9 all-gather.4
